TPU v7x, 256 devices: a whole 4x4x8 slice. The times are simulated.
256 devices in a mesh: grp: 8 (over x, core), lat: 32 (over y, z).
Axes of the slice: x: 4, y: 4, z: 8, core: 2. Of those that a mesh axis runs over, the one named last changes fastest.
Arguments:
- grid_state: bfloat16 [32, 192, 384, 128], P('grp', 'lat'), may hold values from -6 to 6
- noise_field: bfloat16 [32, 192, 384, 128], P('grp', 'lat'), may hold values from -6 to 6
- legendre: bfloat16 [192, 128, 128], P('lat'), may hold values from -0.4375 to 0.4375
- diffusion: float32 [128], replicated, may hold values from 0.1 to 10
- input_weight: bfloat16 [128, 256], replicated, may hold values from -0.5 to 0.5
- noise_weight: bfloat16 [128, 256], replicated, may hold values from -0.5 to 0.5
- input_bias: float32 [256], replicated, may hold values from -4 to 4
- middle_weight: bfloat16 [256, 256], replicated, may hold values from -0.375 to 0.375
- output_weight: bfloat16 [256, 128], replicated, may hold values from -0.375 to 0.375
Outputs:
- new_state: bfloat16 [32, 192, 384, 128], P('grp', 'lat')
- ens_mean: float32 [192, 384, 128], P('lat')
- ens_var: float32 [192, 384, 128], P('lat')
All inputs are finite; a program needn't handle non-finite values.
Results may differ from a plain program's by a relative error of at most 0.012.
Values may be sent and summed in bfloat16 or wider, within the bound.
No kernel may reach another device: no remote copies, remote signals or barrier semaphores. Data moves between devices by JAX's collectives and lax.ppermute only.
A program may use at most 128 MiB of HBM per device.

v0:
```python
import math

import jax
import jax.numpy as jnp
from jax import lax
from jax.sharding import PartitionSpec as P


def total_of_pieces(x, axis):
    return lax.all_gather(x, axis).astype(jnp.float32).sum(0)


def wave_table(lon_count, wave_count):
    lon_ids = jnp.arange(lon_count, dtype=jnp.int32)[:, None]
    wave_ids = jnp.arange(wave_count, dtype=jnp.int32)[None, :]
    phase = (lon_ids * wave_ids % lon_count).astype(jnp.float32) * (2.0 * math.pi / lon_count)
    factor = math.sqrt(2.0 / lon_count)
    joined = jnp.concatenate([jnp.cos(phase), -jnp.sin(phase)], axis=1) * factor
    return joined.astype(jnp.bfloat16)


def damping_filter(diffusion, wave_count):
    degree = jnp.arange(wave_count, dtype=jnp.int32).astype(jnp.float32)
    ratio = degree * (degree + 1.0) / float((wave_count - 1) * wave_count)
    return 1.0 / (1.0 + diffusion[None, :] * (ratio * ratio)[:, None])


def per_device(
    grid_state,
    noise_field,
    legendre,
    diffusion,
    input_weight,
    noise_weight,
    input_bias,
    middle_weight,
    output_weight,
):
    members, lat_rows, lon_count, channels = grid_state.shape
    wave_count = legendre.shape[1]
    local_waves = wave_count // lax.axis_size("lat")
    transform = wave_table(lon_count, wave_count)
    fourier = jnp.einsum(
        "blxc,xk->blkc", grid_state, transform, preferred_element_type=jnp.float32
    ).astype(jnp.bfloat16)
    fourier = fourier.reshape(members, lat_rows, 2, wave_count, channels)
    basis_band = lax.all_to_all(legendre, "lat", split_axis=1, concat_axis=0, tiled=True)
    zonal_ids = lax.axis_index("lat") * local_waves + jnp.arange(local_waves, dtype=jnp.int32)
    total_ids = jnp.arange(wave_count, dtype=jnp.int32)
    triangle = (total_ids[None, :] >= zonal_ids[:, None]).astype(jnp.float32)
    damping = damping_filter(diffusion, wave_count)
    spectrum = jnp.einsum(
        "lmn,blrmc->brmnc",
        basis_band,
        lax.all_to_all(fourier, "lat", split_axis=3, concat_axis=1, tiled=True),
        preferred_element_type=jnp.float32,
    )
    spectrum = spectrum * triangle[None, None, :, :, None]
    filtered = (spectrum * damping[None, None, None, :, :]).astype(jnp.bfloat16)
    banded_grid = jnp.einsum(
        "lmn,brmnc->blrmc", basis_band, filtered, preferred_element_type=jnp.float32
    ).astype(jnp.bfloat16)
    grid_fourier = lax.all_to_all(banded_grid, "lat", split_axis=1, concat_axis=3, tiled=True)
    grid_fourier = grid_fourier.reshape(members, lat_rows, 2 * wave_count, channels)
    smoothed = jnp.einsum(
        "bljc,xj->blxc", grid_fourier, transform, preferred_element_type=jnp.float32
    )
    flat_fields = smoothed.reshape(-1, channels)
    smoothed_in = flat_fields.astype(jnp.bfloat16)
    pre_act = jnp.dot(smoothed_in, input_weight, preferred_element_type=jnp.float32)
    pre_act = pre_act + jnp.dot(
        noise_field.reshape(-1, noise_field.shape[3]),
        noise_weight,
        preferred_element_type=jnp.float32,
    )
    hidden_one = jax.nn.silu(pre_act + input_bias).astype(jnp.bfloat16)
    hidden_two = jax.nn.silu(
        jnp.dot(hidden_one, middle_weight, preferred_element_type=jnp.float32)
    ).astype(jnp.bfloat16)
    tendency = jnp.dot(hidden_two, output_weight, preferred_element_type=jnp.float32)
    new_state = (flat_fields + tendency).astype(jnp.bfloat16).reshape(grid_state.shape)
    member_values = new_state.astype(jnp.float32)
    ensemble = members * lax.axis_size("grp")
    summed = total_of_pieces(jnp.sum(member_values, axis=0).astype(jnp.bfloat16), "grp").astype(
        jnp.float32
    )
    ens_mean = summed / ensemble
    spread = total_of_pieces(
        jnp.sum(jnp.square(member_values - ens_mean), axis=0).astype(jnp.bfloat16), "grp"
    ).astype(jnp.float32)
    ens_var = spread / (ensemble - 1)
    return (new_state, ens_mean, ens_var)


def solution(mesh):
    in_specs = (
        P("grp", "lat", None, None),
        P("grp", "lat", None, None),
        P("lat", None, None),
        P(),
        P(),
        P(),
        P(),
        P(),
        P(),
    )
    out_specs = (P("grp", "lat", None, None), P("lat", None, None), P("lat", None, None))
    return jax.shard_map(
        per_device, mesh=mesh, in_specs=in_specs, out_specs=out_specs, check_vma=False
    )
```

profile of v0, /device:TPU:1, one launch (start us, length us, event | category | flops | bytes accessed | tf_op | source)
XLA Modules:
  0.0 250.5 jit_solution(15547846299608432745)
XLA Ops:
  7.2 1.9 copy.32
  9.1 12.0 %all-to-all-start.1 = ((bf16[6,128,128]{2,0,1:T(8,128)(2,1)}), bf16[6,128,128]{2,0,1:T(8,128)(2,1)S(1)}, u32[]{:S(2)}, u32[]{:S(2)}) async-start(bf16[6,128,128]{2,0,1:T(8,128)(2,1)} %copy.32), calls=%async_computation.1 | async-start | bytes 524288 | tf_op jit(solution)/shard_map/all_to_all | solution.py:47
  21.1 0.8 sine_negate_fusion
  21.9 2.6 %convolution_convert_fusion = bf16[256,4,6,128]{3,0,2,1:T(8,128)(2,1)S(1)} fusion(bf16[4,6,384,128]{3,2,1,0:T(8,128)(2,1)} %param.9, f32[384,128]{0,1:T(8,128)S(1)} %get-tuple-element.3, f32[384,128]{0,1:T(8,128)S(1)} %get-tuple-element.4), kind=kOutput, calls=%fused_computation.13 | convolution fusion | flops 605061120 | bytes 4325376 | tf_op jit(solution)/shard_map/blxc,xk->blkc/dot_general | solution.py:43
  24.6 2.8 %copy.29 = bf16[4,6,2,128,128]{4,2,1,0,3:T(2,128)(2,1)} copy(bf16[4,6,2,128,128]{4,3,2,1,0:T(8,128)(2,1)S(1)} %bitcast.58) | data formatting | bytes 3145728 | tf_op jit(solution)/shard_map/reshape | solution.py:46
  27.4 3.5 %all-to-all-done.1 = bf16[6,128,128]{2,0,1:T(8,128)(2,1)S(1)} async-done(((bf16[6,128,128]{2,0,1:T(8,128)(2,1)}), bf16[6,128,128]{2,0,1:T(8,128)(2,1)S(1)}, u32[]{:S(2)}, u32[]{:S(2)}) %all-to-all-start.1) | async-done | bytes 196640 | tf_op jit(solution)/shard_map/all_to_all | solution.py:47
  30.8 6.5 %all-to-all-start = ((bf16[4,6,2,128,128]{4,2,1,0,3:T(2,128)(2,1)}), bf16[4,6,2,128,128]{4,2,1,0,3:T(2,128)(2,1)}, u32[]{:S(2)}, u32[]{:S(2)}) async-start(bf16[4,6,2,128,128]{4,2,1,0,3:T(2,128)(2,1)} %copy.29), calls=%async_computation | async-start | bytes 3145728 | tf_op jit(solution)/shard_map/all_to_all | solution.py:55
  37.4 0.1 add_divide_fusion
  37.6 36.3 %all-to-all-done = bf16[4,6,2,128,128]{4,2,1,0,3:T(2,128)(2,1)} async-done(((bf16[4,6,2,128,128]{4,2,1,0,3:T(2,128)(2,1)}), bf16[4,6,2,128,128]{4,2,1,0,3:T(2,128)(2,1)}, u32[]{:S(2)}, u32[]{:S(2)}) %all-to-all-start) | async-done | bytes 1572896 | tf_op jit(solution)/shard_map/all_to_all | solution.py:55
  73.9 1.8 copy.30
  75.8 1.7 copy.31
  77.4 3.8 %fusion.5 = bf16[4,192,2,4,128]{4,1,2,0,3:T(8,128)(2,1)} fusion(bf16[4,192,2,4,128]{4,3,2,1,0:T(4,128)(2,1)} %bitcast.62, f32[128,128]{0,1:T(8,128)S(1)} %add_divide_fusion, f32[4,128]{1,0:T(4,128)S(1)} %fusion.23, bf16[192,4,128,1,1]{2,1,0,4,3:T(4,128)(2,1)S(1)} %bitcast.64), kind=kOutput, calls=%fused_computation.16 | convolution fusion | flops 405012480 | bytes 3409920 | tf_op jit(solution)/shard_map/lmn,brmnc->blrmc/dot_general | solution.py:60
  81.2 3.0 %copy.38 = bf16[4,192,2,4,128]{4,2,0,3,1:T(2,128)(2,1)S(1)} copy(bf16[4,192,2,4,128]{4,1,2,0,3:T(8,128)(2,1)} %fusion.5) | data formatting | bytes 3145728 | tf_op jit(solution)/shard_map/convert_element_type | solution.py:62
  84.3 43.7 %all_to_all.51 = bf16[4,192,2,4,128]{4,2,0,3,1:T(2,128)(2,1)S(1)} all-to-all(bf16[4,192,2,4,128]{4,2,0,3,1:T(2,128)(2,1)S(1)} %copy.38), channel_id=1, replica_groups=mesh['grp'=8,'lat'=32] {'lat'}, dimensions={1} | all-to-all | bytes 3145728 | tf_op jit(solution)/shard_map/all_to_all | solution.py:63
  128.0 0.8 copy.39
  128.8 0.9 copy.40
  129.7 0.8 fusion.21
  130.5 2.2 copy-done.1
  132.7 0.3 bitcast_convert_fusion
  132.9 0.6 copy-done.4
  133.5 5.0 %fusion.32 = f32[9216,256]{1,0:T(8,128)} fusion(bf16[9216,128]{1,0:T(8,128)(2,1)S(1)} %bitcast_convert_fusion, bf16[128,256]{1,0:T(8,128)(2,1)S(1)} %copy-done.4), kind=kOutput, calls=%fused_computation.48 | convolution fusion | flops 603979776 | bytes 11862016 | tf_op jit(solution)/shard_map/dot_general | solution.py:70
  138.6 7.6 %fusion.2 = f32[9216,256]{1,0:T(8,128)} fusion(bf16[256,256]{1,0:T(8,128)(2,1)S(1)} %copy-done.6, f32[9216,256]{1,0:T(8,128)} %fusion.32, bf16[9216,128]{1,0:T(8,128)(2,1)S(1)} %bitcast.51, bf16[128,256]{1,0:T(8,128)(2,1)S(1)} %copy-done.7, f32[256]{0:T(256)S(1)} %copy-done.9), kind=kOutput, calls=%fused_computation.10 | convolution fusion | flops 1828454400 | bytes 21431296 | tf_op jit(solution)/shard_map/dot_general | solution.py:78
  146.2 9.1 %fusion.1 = bf16[9216,128]{1,0:T(8,128)(2,1)} fusion(f32[9216,128]{1,0:T(8,128)} %bitcast.52, bf16[256,128]{1,0:T(8,128)(2,1)S(1)} %copy-done.8, f32[9216,256]{1,0:T(8,128)} %fusion.2), kind=kOutput, calls=%fused_computation.3 | convolution fusion | flops 618135552 | bytes 16580608 | tf_op jit(solution)/shard_map/dot_general | solution.py:80
  155.2 3.0 %reduce_sum.39 = bf16[6,384,128]{2,1,0:T(8,128)(2,1)} reduce(bf16[4,6,384,128]{3,2,1,0:T(8,128)(2,1)} %bitcast.53, bf16[]{:T(256)} %constant.37.clone.1), dimensions={0}, to_apply=%region_0.1 | reduce | flops 884736 | bytes 2949122 | tf_op jit(solution)/shard_map/reduce_sum | solution.py:84
  158.3 37.7 %all-gather.5.cloned.1.call-done = bf16[48,384,128]{2,1,0:T(8,128)(2,1)} async-done(((bf16[6,384,128]{2,1,0:T(8,128)(2,1)}), bf16[48,384,128]{2,1,0:T(8,128)(2,1)}) %all-gather.5.cloned.1.call-update) | async-done | bytes 4718608 | tf_op jit(solution)/shard_map/all_gather | solution.py:10
  196.0 3.2 %convert_reduce_fusion.1 = f32[6,384,128]{2,1,0:T(8,128)S(1)} fusion(bf16[8,6,384,128]{3,2,1,0:T(8,128)(2,1)} %bitcast.60), kind=kLoop, calls=%fused_computation.5 | loop fusion | flops 4423680 | bytes 5898240 | tf_op jit(solution)/shard_map/reduce_sum | solution.py:10
  199.2 0.1 broadcast_multiply_fusion.1
  199.3 1.6 copy-done.2
  200.9 1.5 multiply_reduce_fusion
  202.5 36.9 %all-gather.7.cloned.1.call-done = bf16[48,384,128]{2,1,0:T(8,128)(2,1)} async-done(((bf16[6,384,128]{2,1,0:T(8,128)(2,1)}), bf16[48,384,128]{2,1,0:T(8,128)(2,1)}) %all-gather.7.cloned.1.call-update) | async-done | bytes 4718608 | tf_op jit(solution)/shard_map/all_gather | solution.py:10
  239.4 3.2 %convert_reduce_fusion = f32[6,384,128]{2,1,0:T(8,128)S(1)} fusion(bf16[8,6,384,128]{3,2,1,0:T(8,128)(2,1)} %bitcast.61), kind=kLoop, calls=%fused_computation.4 | loop fusion | flops 4423680 | bytes 5898240 | tf_op jit(solution)/shard_map/reduce_sum | solution.py:10
  242.6 1.1 broadcast_multiply_fusion
  (25 shorter events, 0.3 us)
Async XLA Ops:
  7.2 131.4 %copy-start = (bf16[4,6,384,128]{3,2,1,0:T(8,128)(2,1)S(1)}, bf16[4,6,384,128]{3,2,1,0:T(8,128)(2,1)}, u32[]{:S(2)}) copy-start(bf16[4,6,384,128]{3,2,1,0:T(8,128)(2,1)} %param.10) | copy-start | bytes 7077892
  9.1 21.7 %all-to-all-start.1 = ((bf16[6,128,128]{2,0,1:T(8,128)(2,1)}), bf16[6,128,128]{2,0,1:T(8,128)(2,1)S(1)}, u32[]{:S(2)}, u32[]{:S(2)}) async-start(bf16[6,128,128]{2,0,1:T(8,128)(2,1)} %copy.32), calls=%async_computation.1 | async-start | bytes 524288 | tf_op jit(solution)/shard_map/all_to_all | solution.py:47
  27.4 10.1 %copy-start.5 = (f32[128]{0:T(128)S(1)}, f32[128]{0:T(128)}, u32[]{:S(2)}) copy-start(f32[128]{0:T(128)} %param.12) | copy-start | bytes 1540
  30.8 43.1 %all-to-all-start = ((bf16[4,6,2,128,128]{4,2,1,0,3:T(2,128)(2,1)}), bf16[4,6,2,128,128]{4,2,1,0,3:T(2,128)(2,1)}, u32[]{:S(2)}, u32[]{:S(2)}) async-start(bf16[4,6,2,128,128]{4,2,1,0,3:T(2,128)(2,1)} %copy.29), calls=%async_computation | async-start | bytes 3145728 | tf_op jit(solution)/shard_map/all_to_all | solution.py:55
  37.3 158.8 %all-gather.5.cloned.1.call-start = ((), (), s32[]{:S(2)}) async-start(), calls=%async_computation.3 | async-start | bytes 5308416 | tf_op jit(solution)/shard_map/all_gather | solution.py:10
  130.5 2.2 copy-start.1
  132.7 0.8 copy-start.4
  133.5 5.0 %copy-start.6 = (bf16[256,256]{1,0:T(8,128)(2,1)S(1)}, bf16[256,256]{1,0:T(8,128)(2,1)}, u32[]{:S(2)}) copy-start(bf16[256,256]{1,0:T(8,128)(2,1)} %param.16) | copy-start | bytes 393220
  133.5 5.0 %copy-start.7 = (bf16[128,256]{1,0:T(8,128)(2,1)S(1)}, bf16[128,256]{1,0:T(8,128)(2,1)}, u32[]{:S(2)}) copy-start(bf16[128,256]{1,0:T(8,128)(2,1)} %param.14) | copy-start | bytes 196612
  133.5 5.0 %copy-start.9 = (f32[256]{0:T(256)S(1)}, f32[256]{0:T(256)}, u32[]{:S(2)}) copy-start(f32[256]{0:T(256)} %param.15) | copy-start | bytes 3076
  138.5 7.6 %copy-start.8 = (bf16[256,128]{1,0:T(8,128)(2,1)S(1)}, bf16[256,128]{1,0:T(8,128)(2,1)}, u32[]{:S(2)}) copy-start(bf16[256,128]{1,0:T(8,128)(2,1)} %param.17) | copy-start | bytes 196612
  158.3 81.1 %all-gather.7.cloned.1.call-start = ((), (), s32[]{:S(2)}) async-start(), calls=%async_computation.4 | async-start | bytes 5308416 | tf_op jit(solution)/shard_map/all_gather | solution.py:10
  199.2 1.7 copy-start.2
  200.9 1.6 copy-start.3
Sparse Core Ops, SparseCore 0:
  158.4 37.5 all-gather.4
  202.6 36.7 all-gather.6
where the time goes:
time: 251 us
  waiting for transfers between devices  114 us (45%)
  blocking collectives  43.7 us (17%)
  matrix products  29 us (12%)
  starting transfers between devices  18.6 us (7%)
  local copies, waits for them, and re-layouts  17.3 us (7%)
  between operations  14.2 us (6%)
  other arithmetic  13.3 us (5%)
    all_gather x2, waiting for transfers between devices, total_of_pieces(): return lax.all_gather(x, axis).astype(jnp.float32).sum(0)  74.7 us
    all_to_all x1, blocking collectives, per_device(): lax.all_to_all(banded_grid, 'lat', split_axis=1, concat_axis=3, tiled=True)  43.7 us
    all_to_all x1, waiting for transfers between devices, per_device(): lax.all_to_all(fourier, 'lat', split_axis=3, concat_axis=1, tiled=True)  36.3 us
    all_to_all x1, starting transfers between devices, per_device(): lax.all_to_all(legendre, 'lat', split_axis=1, concat_axis=0, tiled=True)  12 us
    dot_general x1, matrix products, per_device(): jnp.dot(hidden_two, output_weight, preferred_element_type=jnp.float32)  9.08 us
    dot_general x1, matrix products, per_device(): jnp.dot(hidden_one, middle_weight, preferred_element_type=jnp.float32)  7.59 us
    all_to_all x1, starting transfers between devices, per_device(): lax.all_to_all(fourier, 'lat', split_axis=3, concat_axis=1, tiled=True)  6.47 us
    reduce_sum x2, other arithmetic, total_of_pieces(): return lax.all_gather(x, axis).astype(jnp.float32).sum(0)  6.35 us
  transfers between devices with their start and end apart: 4, of which 4 were waited for; matrix products, arithmetic and copies ran while one was open for 3% of the time, Pallas kernels for 0%

commit v1 on v0

v1 whole, which is shorter than its diff:
```python
import math

import jax
import jax.numpy as jnp
import numpy as np
from jax import lax
from jax.experimental import pallas as pl
from jax.experimental.pallas import tpu as pltpu
from jax.sharding import PartitionSpec as P

BF = jnp.bfloat16
F32 = jnp.float32


def wave_table(lon_count, wave_count):
    lon_ids = np.arange(lon_count)[:, None]
    wave_ids = np.arange(wave_count)[None, :]
    phase = (lon_ids * wave_ids % lon_count) * (2.0 * math.pi / lon_count)
    factor = math.sqrt(2.0 / lon_count)
    return np.concatenate([np.cos(phase), -np.sin(phase)], axis=1) * factor


def paired_table(lon_count, wave_count, owners):
    local = wave_count // owners
    table = wave_table(lon_count, wave_count).T.reshape(2, owners, 1, local, 1, lon_count)
    same = np.eye(2).reshape(1, 1, 2, 1, 2, 1)
    return (table * same).reshape(2 * wave_count * 2, 2 * lon_count)


def pair_order(wave_count, owners):
    local = wave_count // owners
    eye = np.eye(wave_count).reshape(owners, 1, local, 1, wave_count)
    same = np.eye(2).reshape(1, 2, 1, 2, 1)
    return (eye * same).reshape(2 * wave_count, 2 * wave_count)


def forward_kernel(grid_ref, legendre_ref, table_ref, order_ref, out_ref):
    owners, rows, _ = out_ref.shape
    half = pl.program_id(1)
    lon = grid_ref.shape[2]
    chan = grid_ref.shape[3]
    fields = jnp.concatenate(
        [grid_ref[0].reshape(2 * lon, chan), grid_ref[1].reshape(2 * lon, chan)], axis=1
    )
    coeffs = jnp.dot(table_ref[...], fields, preferred_element_type=F32).astype(BF)
    waves = coeffs.shape[0] // 2
    width = 2 * chan
    base = pl.multiple_of(half * (2 * width), 2 * width)
    out_ref[:, :, pl.ds(base, width)] = coeffs[:waves].reshape(owners, rows, width)
    out_ref[:, :, pl.ds(base + width, width)] = coeffs[waves:].reshape(owners, rows, width)

    @pl.when(half == 0)
    def _():
        basis = legendre_ref[...].reshape(-1, legendre_ref.shape[2])
        moved = jnp.dot(order_ref[...], basis, preferred_element_type=F32).astype(BF)
        out_ref[:, :, 4 * width :] = moved.reshape(owners, rows, legendre_ref.shape[2])


def spectral_kernel(first_ref, in_ref, basis_ref, diffusion_ref, out_ref, table_ref, damp_ref):
    owners, rows, width = in_ref.shape
    total = basis_ref.shape[2]
    local = table_ref.shape[1] // total

    @pl.when(pl.program_id(0) == 0)
    def _():
        basis = basis_ref[...].reshape(owners * rows, total)
        row_ids = lax.broadcasted_iota(jnp.int32, basis.shape, 0) % local
        total_ids = lax.broadcasted_iota(jnp.int32, basis.shape, 1)
        for m in range(local):
            keep = (row_ids == m) & (total_ids >= first_ref[0] + m)
            table_ref[:, m * total : (m + 1) * total] = jnp.where(keep, basis, jnp.zeros_like(basis))
        degree = lax.broadcasted_iota(jnp.int32, damp_ref.shape, 0).astype(F32)
        ratio = degree * (degree + 1.0) / float((total - 1) * total)
        damp_ref[...] = 1.0 / (1.0 + diffusion_ref[...] * (ratio * ratio))

    values = in_ref[...].reshape(owners * rows, width)
    table = table_ref[...]
    spectrum = lax.dot_general(
        table, values, (((0,), (0,)), ((), ())), preferred_element_type=F32
    )
    damping = damp_ref[...]
    chan = damping.shape[1]
    columns = [
        jnp.concatenate(
            [
                (spectrum[m * total : (m + 1) * total, k * chan : (k + 1) * chan] * damping).astype(BF)
                for m in range(local)
            ],
            axis=0,
        )
        for k in range(width // chan)
    ]
    filtered = jnp.concatenate(columns, axis=1)
    back = jnp.dot(table, filtered, preferred_element_type=F32).astype(BF)
    out_ref[...] = back.reshape(owners, rows, width)


def silu(v):
    u = 0.5 * v
    return u + u * jnp.tanh(u)


def column_kernel(
    core_ref,
    in_ref,
    noise_ref,
    table_ref,
    first_weight_ref,
    bias_ref,
    middle_ref,
    output_ref,
    state_ref,
    keep_ref,
    send_ref,
    sum_ref,
    dev_ref,
    moment_ref,
):
    owners, rows, width = in_ref.shape
    lon = noise_ref.shape[2]
    chan = noise_ref.shape[3]
    half = pl.program_id(1)
    coeffs = in_ref[...].reshape(owners * rows, width)
    stacked = jnp.concatenate([coeffs[:, : width // 2], coeffs[:, width // 2 :]], axis=0)
    smoothed = jnp.dot(table_ref[...], stacked, preferred_element_type=F32)
    values = []
    for b in range(2):
        fields = smoothed[:, b * chan : (b + 1) * chan]
        noise = noise_ref[b].reshape(2 * lon, chan)
        joined = jnp.concatenate([fields.astype(BF), noise], axis=1)
        hidden = silu(
            jnp.dot(joined, first_weight_ref[...], preferred_element_type=F32) + bias_ref[...]
        ).astype(BF)
        hidden = silu(jnp.dot(hidden, middle_ref[...], preferred_element_type=F32)).astype(BF)
        tendency = jnp.dot(hidden, output_ref[...], preferred_element_type=F32)
        state = (fields + tendency).astype(BF)
        state_ref[b] = state.reshape(2, lon, chan)
        values.append(state.astype(F32))
    pair_sum = values[0] + values[1]
    gap = values[0] - values[1]
    pair_dev = 0.5 * (gap * gap)

    @pl.when(half == 0)
    def _():
        sum_ref[...] = pair_sum
        dev_ref[...] = pair_dev

    @pl.when(half == 1)
    def _():
        other = sum_ref[...]
        total = (pair_sum + other).astype(BF)
        change = pair_sum - other
        dev = (pair_dev + dev_ref[...] + 0.25 * (change * change)).astype(BF)
        parts = keep_ref.shape[0]
        piece = keep_ref.shape[3]
        for l in range(2):
            for h in range(2):
                for q in range(parts):
                    at = l * lon + (h * parts + q) * piece
                    moment_ref[h, q, 0, l] = total[at : at + piece]
                    moment_ref[h, q, 1, l] = dev[at : at + piece]
        keep_ref[...] = moment_ref[core_ref[0]]
        send_ref[...] = moment_ref[1 - core_ref[0]]


def per_device(
    grid_state,
    noise_field,
    legendre,
    diffusion,
    input_weight,
    noise_weight,
    input_bias,
    middle_weight,
    output_weight,
):
    members, lat_rows, lon, chan = grid_state.shape
    waves, total = legendre.shape[1:]
    owners = lax.axis_size("lat")
    groups = lax.axis_size("grp")
    chips = groups // 2
    local = waves // owners
    pairs = lat_rows // 2
    rows = 2 * local
    hidden = middle_weight.shape[0]
    lanes = members * 2 * chan
    table = jnp.asarray(paired_table(lon, waves, owners), dtype=BF)
    back_table = jnp.asarray(paired_table(lon, waves, owners).T, dtype=BF)
    order = jnp.asarray(pair_order(waves, owners), dtype=BF)
    whole = lambda *shape: pl.BlockSpec(shape, lambda *_: (0,) * len(shape))
    scalar = pl.BlockSpec(memory_space=pltpu.SMEM)

    outgoing = pl.pallas_call(
        forward_kernel,
        grid=(pairs, members // 2),
        in_specs=[
            pl.BlockSpec((2, 2, lon, chan), lambda p, h: (h, p, 0, 0)),
            pl.BlockSpec((2, waves, total), lambda p, h: (p, 0, 0)),
            whole(*table.shape),
            whole(*order.shape),
        ],
        out_specs=pl.BlockSpec((owners, rows, lanes + total), lambda p, h: (0, p, 0)),
        out_shape=jax.ShapeDtypeStruct((owners, pairs * rows, lanes + total), BF),
        name="forward",
    )(grid_state, legendre, table, order)
    incoming = lax.all_to_all(outgoing, "lat", 0, 0, tiled=True)

    first = (lax.axis_index("lat") * local).astype(jnp.int32).reshape(1)
    width = 2 * chan
    banded = pl.pallas_call(
        spectral_kernel,
        grid=(lanes // width,),
        in_specs=[
            scalar,
            pl.BlockSpec((owners, pairs * rows, width), lambda i: (0, 0, i)),
            pl.BlockSpec((owners, pairs * rows, total), lambda i: (0, 0, lanes // total)),
            whole(1, chan),
        ],
        out_specs=pl.BlockSpec((owners, pairs * rows, width), lambda i: (0, 0, i)),
        out_shape=jax.ShapeDtypeStruct((owners, pairs * rows, lanes), BF),
        scratch_shapes=[
            pltpu.VMEM((owners * pairs * rows, local * total), BF),
            pltpu.VMEM((total, chan), F32),
        ],
        name="spectral",
    )(first, incoming, incoming, diffusion.reshape(1, chan))
    returned = lax.all_to_all(banded, "lat", 0, 0, tiled=True)

    core = (lax.axis_index("grp") % 2).astype(jnp.int32).reshape(1)
    first_weight = jnp.concatenate([input_weight, noise_weight], axis=0)
    piece = lon // (2 * chips)
    moment_shape = (chips, 2, lat_rows, piece, chan)
    moment_block = (chips, 2, 2, piece, chan)
    moment_spec = pl.BlockSpec(moment_block, lambda p, h: (0, 0, p, 0, 0))
    new_state, keep, send = pl.pallas_call(
        column_kernel,
        grid=(pairs, members // 2),
        in_specs=[
            scalar,
            pl.BlockSpec((owners, rows, 4 * chan), lambda p, h: (0, p, h)),
            pl.BlockSpec((2, 2, lon, chan), lambda p, h: (h, p, 0, 0)),
            whole(*back_table.shape),
            whole(2 * chan, hidden),
            whole(1, hidden),
            whole(hidden, hidden),
            whole(hidden, chan),
        ],
        out_specs=[
            pl.BlockSpec((2, 2, lon, chan), lambda p, h: (h, p, 0, 0)),
            moment_spec,
            moment_spec,
        ],
        out_shape=[
            jax.ShapeDtypeStruct(grid_state.shape, BF),
            jax.ShapeDtypeStruct(moment_shape, BF),
            jax.ShapeDtypeStruct(moment_shape, BF),
        ],
        scratch_shapes=[
            pltpu.VMEM((2 * lon, chan), F32),
            pltpu.VMEM((2 * lon, chan), F32),
            pltpu.VMEM((2,) + moment_block, BF),
        ],
        name="column",
    )(
        core,
        returned,
        noise_field,
        back_table,
        first_weight,
        input_bias.reshape(1, hidden),
        middle_weight,
        output_weight,
    )

    swap = [(i, i ^ 1) for i in range(groups)]
    lines = [list(range(k, groups, 2)) for k in range(2)]
    got = lax.ppermute(send, "grp", swap).astype(F32)
    kept = keep.astype(F32)
    change = kept[:, 0] - got[:, 0]
    chip_sum = kept[:, 0] + got[:, 0]
    chip_members = 2 * members
    chip_dev = kept[:, 1] + got[:, 1] + change * change / chip_members
    chip_moments = jnp.stack([chip_sum, chip_dev], axis=1).astype(BF)
    gathered = lax.all_to_all(
        chip_moments, "grp", 0, 0, tiled=True, axis_index_groups=lines
    ).astype(F32)
    sums = gathered[:, 0]
    whole_sum = sums.sum(0)
    shift = sums - (whole_sum / chips)[None]
    devs = gathered[:, 1].sum(0) + (shift * shift).sum(0) / chip_members
    ensemble = members * groups
    result = jnp.stack([whole_sum / ensemble, devs / (ensemble - 1)]).astype(BF)
    mine = lax.all_gather(result, "grp", axis=0, axis_index_groups=lines)
    other = lax.ppermute(mine, "grp", swap)
    low = jnp.where(core[0] == 0, mine, other)
    high = jnp.where(core[0] == 0, other, mine)
    both = jnp.stack([low, high])
    out = both.transpose(2, 3, 0, 1, 4, 5).reshape(2, lat_rows, lon, chan).astype(F32)
    return (new_state, out[0], out[1])


def solution(mesh):
    in_specs = (
        P("grp", "lat", None, None),
        P("grp", "lat", None, None),
        P("lat", None, None),
        P(),
        P(),
        P(),
        P(),
        P(),
        P(),
    )
    out_specs = (P("grp", "lat", None, None), P("lat", None, None), P("lat", None, None))
    return jax.shard_map(
        per_device, mesh=mesh, in_specs=in_specs, out_specs=out_specs, check_vma=False
    )
```

time: 251 us -> 164 us (0.65)
  waiting for transfers between devices: 114 us -> 80.5 us
  matrix products: 29 us -> 0 us
  Pallas kernels: 0 us -> 25 us
  blocking collectives: 43.7 us -> 24.4 us
  between operations: 14.2 us -> 0.78 us
  local copies, waits for them, and re-layouts: 17.3 us -> 3.97 us
  other arithmetic: 13.3 us -> 2.66 us
  starting transfers between devices: 18.6 us -> 26.7 us
    all_gather x2 -> x0, waiting for transfers between devices: 74.7 us -> none  [total_of_pieces(): return lax.all_gather(x, axis).astype(jnp.float32).sum(0)]
    all_to_all x2, waiting for transfers between devices: 39.8 us -> 78.1 us  [the longest x1 41.9 us: per_device(): incoming = lax.all_to_all(outgoing, 'lat', 0, 0, tiled=True)]
    all_to_all x1, blocking collectives: 43.7 us -> 13.4 us  [per_device(): lax.all_to_all(chip_moments, 'grp', 0, 0, tiled=True, axis_index_groups=l...]
    dot_general x6 -> x0, matrix products: 29 us -> none  [the longest x1 9.08 us: per_device(): jnp.dot(hidden_two, output_weight, preferred_element_type=jnp.float32)]
    pallas_call x0 -> x3, Pallas kernels: none -> 25 us  [the longest x1 12 us: per_device(): pl.pallas_call(column_kernel, grid=(pairs, members // 2), in_specs=[scala...]
    all_gather x0 -> x1, blocking collectives: none -> 10.9 us  [per_device(): mine = lax.all_gather(result, 'grp', axis=0, axis_index_groups=lines)]
    reduce_sum x4 -> x2, other arithmetic: 10.9 us -> 0.12 us  [the longest x1 0.06 us: per_device(): devs = gathered[:, 1].sum(0) + (shift * shift).sum(0) / chip_members]
    ppermute x0 -> x2, starting transfers between devices: none -> 7.76 us  [the longest x1 4.33 us: per_device(): other = lax.ppermute(mine, 'grp', swap)]
  transfers between devices with their start and end apart: 4 -> 4, of which waited for: 4 -> 4; matrix products, arithmetic and copies ran while one was open for 3% -> 1% of each run, Pallas kernels for 0% -> 0%
where the time goes in v1:
time: 164 us
  waiting for transfers between devices  80.5 us (49%)
  starting transfers between devices  26.7 us (16%)
  Pallas kernels  25 us (15%)
  blocking collectives  24.4 us (15%)
  local copies, waits for them, and re-layouts  3.97 us (2%)
  other arithmetic  2.66 us (2%)
    all_to_all x1, waiting for transfers between devices, per_device(): incoming = lax.all_to_all(outgoing, 'lat', 0, 0, tiled=True)  41.9 us
    all_to_all x1, waiting for transfers between devices, per_device(): returned = lax.all_to_all(banded, 'lat', 0, 0, tiled=True)  36.2 us
    all_to_all x1, blocking collectives, per_device(): lax.all_to_all(chip_moments, 'grp', 0, 0, tiled=True, axis_index_groups=l...  13.4 us
    pallas_call x1, Pallas kernels, per_device(): pl.pallas_call(column_kernel, grid=(pairs, members // 2), in_specs=[scala...  12 us
    all_to_all x1, starting transfers between devices, per_device(): incoming = lax.all_to_all(outgoing, 'lat', 0, 0, tiled=True)  12 us
    all_gather x1, blocking collectives, per_device(): mine = lax.all_gather(result, 'grp', axis=0, axis_index_groups=lines)  10.9 us
    all_to_all x1, starting transfers between devices, per_device(): returned = lax.all_to_all(banded, 'lat', 0, 0, tiled=True)  6.88 us
    pallas_call x1, Pallas kernels, per_device(): pl.pallas_call(spectral_kernel, grid=(lanes // width,), in_specs=[scalar,...  6.54 us
  transfers between devices with their start and end apart: 4, of which 4 were waited for; matrix products, arithmetic and copies ran while one was open for 1% of the time, Pallas kernels for 0%

profile of v1, /device:TPU:1, one launch (start us, length us, event | category | flops | bytes accessed | tf_op | source)
XLA Modules:
  0.0 163.8 jit_solution(15744466215441791000)
XLA Ops:
  0.6 6.4 %forward.1 = bf16[32,24,1152]{2,1,0:T(8,128)(2,1)} custom-call(bf16[4,6,384,128]{3,2,1,0:T(8,128)(2,1)} %grid_ref.1, bf16[6,128,128]{2,1,0:T(8,128)(2,1)} %legendre_ref.1, bf16[512,768]{1,0:T(8,128)(2,1)} %constant.47.clone.table_ref, bf16[256,256]{1,0:T(8,128)(2,1)} %constant.49.clone.order_ref), custom_call_target="tpu_custom_call" | custom-call | tf_op jit(solution)/shard_map/forward/pallas_call | solution.py:193
  7.0 12.0 %all-to-all-start = ((bf16[32,24,1152]{2,1,0:T(8,128)(2,1)}), bf16[32,24,1152]{2,1,0:T(8,128)(2,1)S(1)}, u32[]{:S(2)}, u32[]{:S(2)}) async-start(bf16[32,24,1152]{2,1,0:T(8,128)(2,1)} %forward.1), calls=%async_computation | async-start | bytes 3538944 | tf_op jit(solution)/shard_map/all_to_all | solution.py:206
  19.1 41.9 %all-to-all-done.in_ref.basis_ref = bf16[32,24,1152]{2,1,0:T(8,128)(2,1)S(1)} async-done(((bf16[32,24,1152]{2,1,0:T(8,128)(2,1)}), bf16[32,24,1152]{2,1,0:T(8,128)(2,1)S(1)}, u32[]{:S(2)}, u32[]{:S(2)}) %all-to-all-start) | async-done | bytes 1769504 | tf_op jit(solution)/shard_map/all_to_all | solution.py:206
  61.0 0.0 copy-start
  61.0 1.2 copy-done
  62.2 6.5 %spectral.1 = bf16[32,24,1024]{2,1,0:T(8,128)(2,1)} custom-call(s32[1]{0:T(128)} %bitcast.1.first_ref, bf16[32,24,1152]{2,1,0:T(8,128)(2,1)} %copy-done, bf16[32,24,1152]{2,1,0:T(8,128)(2,1)} %copy-done, f32[1,128]{1,0:T(1,128)} %bitcast.27), custom_call_target="tpu_custom_call" | custom-call | tf_op jit(solution)/shard_map/spectral/pallas_call | solution.py:210
  68.7 0.0 copy-start.2
  68.7 0.0 copy-start.3
  68.7 6.9 %all-to-all-start.1 = ((bf16[32,24,1024]{2,1,0:T(8,128)(2,1)}), bf16[32,24,1024]{2,1,0:T(8,128)(2,1)S(1)}, u32[]{:S(2)}, u32[]{:S(2)}) async-start(bf16[32,24,1024]{2,1,0:T(8,128)(2,1)} %spectral.1), calls=%async_computation.1 | async-start | bytes 3145728 | tf_op jit(solution)/shard_map/all_to_all | solution.py:227
  75.6 0.0 copy-done.2
  75.6 0.0 copy-done.3
  75.6 0.7 pad_maximum_fusion.2.first_weight_ref
  76.3 36.2 %all-to-all-done.1.in_ref = bf16[32,24,1024]{2,1,0:T(8,128)(2,1)S(1)} async-done(((bf16[32,24,1024]{2,1,0:T(8,128)(2,1)}), bf16[32,24,1024]{2,1,0:T(8,128)(2,1)S(1)}, u32[]{:S(2)}, u32[]{:S(2)}) %all-to-all-start.1) | async-done | bytes 1572896 | tf_op jit(solution)/shard_map/all_to_all | solution.py:227
  112.5 1.1 copy-done.1
  113.7 12.0 %column.1 = (bf16[4,6,384,128]{3,2,1,0:T(8,128)(2,1)}, bf16[4,2,6,48,128]{4,3,2,1,0:T(8,128)(2,1)}, bf16[4,2,6,48,128]{4,3,2,1,0:T(8,128)(2,1)}) custom-call(s32[1]{0:T(128)} %bitcast.core_ref, bf16[32,24,1024]{2,1,0:T(8,128)(2,1)} %copy-done.1, bf16[4,6,384,128]{3,2,1,0:T(8,128)(2,1)} %noise_ref.1, bf16[768,512]{1,0:T(8,128)(2,1)} %constant.48.clone.table_ref, ...), custom_call_target="tpu_custom_call" | custom-call | tf_op jit(solution)/shard_map/column/pallas_call | solution.py:235
  125.7 3.4 %collective-permute-start = (bf16[4,2,6,48,128]{4,3,2,1,0:T(8,128)(2,1)}, bf16[4,2,6,48,128]{4,3,2,1,0:T(8,128)(2,1)S(1)}, u32[]{:S(2)}, u32[]{:S(2)}) collective-permute-start(bf16[4,2,6,48,128]{4,3,2,1,0:T(8,128)(2,1)} %get-tuple-element.8), channel_id=1, source_target_pairs={{0,32},{32,0},{64,96},{96,64},{128,160},{160,128},{192,224},{224,1... | collective-permute-start | bytes 1769480 | tf_op jit(solution)/shard_map/ppermute | solution.py:277
  129.1 1.2 convert_element_type.25
  130.3 0.7 collective-permute-done
  131.0 0.1 convert_element_type.26
  131.1 0.2 add_convert_fusion
  131.3 0.1 pad_maximum_fusion
  131.3 13.4 %all_to_all.15 = bf16[4,2,6,48,128]{4,3,2,1,0:T(8,128)(2,1)S(1)} all-to-all(bf16[4,2,6,48,128]{4,3,2,1,0:T(8,128)(2,1)S(1)} %pad_maximum_fusion), channel_id=1, replica_groups={{0,64,128,192},{32,96,160,224},{1,65,129,193},{33,97,161,225},{2,66,130..., dimensions={0} | all-to-all | bytes 1179648 | tf_op jit(solution)/shard_map/all_to_all | solution.py:284
  144.8 0.1 convert_element_type.27
  144.9 0.1 slice_reduce_fusion.1
  145.0 0.1 fusion.3
  145.1 10.9 %all_gather.4 = bf16[4,2,6,48,128]{4,3,2,1,0:T(8,128)(2,1)S(1)} all-gather(bf16[1,2,6,48,128]{4,3,2,1,0:T(8,128)(2,1)S(1)} %pad_maximum_fusion.1), channel_id=1, replica_groups={{0,64,128,192},{32,96,160,224},{1,65,129,193},{33,97,161,225},{2,66,130..., dimensions={0}, use_global_device_ids=true | all-gather | bytes 737280 | tf_op jit(solution)/shard_map/all_gather | solution.py:293
  156.0 0.1 copy.18
  156.1 4.3 %collective-permute-start.1 = (bf16[4,2,6,48,128]{4,3,0,2,1:T(8,128)(2,1)S(1)}, bf16[4,2,6,48,128]{4,3,0,2,1:T(8,128)(2,1)S(1)}, u32[]{:S(2)}, u32[]{:S(2)}) collective-permute-start(bf16[4,2,6,48,128]{4,3,0,2,1:T(8,128)(2,1)S(1)} %copy.18), channel_id=1, source_target_pairs={{0,32},{32,0},{64,96},{96,64},{128,160},{160,128},{192,224},{224,1... | collective-permute-start | bytes 1769480 | tf_op jit(solution)/shard_map/ppermute | solution.py:294
  160.4 1.6 collective-permute-done.1
  162.0 0.1 select_bitcast_fusion.1
  162.1 0.2 convert_bitcast_fusion
  162.3 1.6 fusion.6
  (4 shorter events, 0.1 us)
Async XLA Ops:
  7.0 53.9 %all-to-all-start = ((bf16[32,24,1152]{2,1,0:T(8,128)(2,1)}), bf16[32,24,1152]{2,1,0:T(8,128)(2,1)S(1)}, u32[]{:S(2)}, u32[]{:S(2)}) async-start(bf16[32,24,1152]{2,1,0:T(8,128)(2,1)} %forward.1), calls=%async_computation | async-start | bytes 3538944 | tf_op jit(solution)/shard_map/all_to_all | solution.py:206
  61.0 1.2 copy-start
  68.7 6.9 %copy-start.2 = (bf16[128,256]{1,0:T(8,128)(2,1)S(1)}, bf16[128,256]{1,0:T(8,128)(2,1)}, u32[]{:S(2)}) copy-start(bf16[128,256]{1,0:T(8,128)(2,1)} %param.17) | copy-start | bytes 196612
  68.7 6.9 %copy-start.3 = (bf16[128,256]{1,0:T(8,128)(2,1)S(1)}, bf16[128,256]{1,0:T(8,128)(2,1)}, u32[]{:S(2)}) copy-start(bf16[128,256]{1,0:T(8,128)(2,1)} %param.16) | copy-start | bytes 196612
  68.7 43.8 %all-to-all-start.1 = ((bf16[32,24,1024]{2,1,0:T(8,128)(2,1)}), bf16[32,24,1024]{2,1,0:T(8,128)(2,1)S(1)}, u32[]{:S(2)}, u32[]{:S(2)}) async-start(bf16[32,24,1024]{2,1,0:T(8,128)(2,1)} %spectral.1), calls=%async_computation.1 | async-start | bytes 3145728 | tf_op jit(solution)/shard_map/all_to_all | solution.py:227
  112.5 1.1 copy-start.1
  125.7 5.3 %collective-permute-start = (bf16[4,2,6,48,128]{4,3,2,1,0:T(8,128)(2,1)}, bf16[4,2,6,48,128]{4,3,2,1,0:T(8,128)(2,1)S(1)}, u32[]{:S(2)}, u32[]{:S(2)}) collective-permute-start(bf16[4,2,6,48,128]{4,3,2,1,0:T(8,128)(2,1)} %get-tuple-element.8), channel_id=1, source_target_pairs={{0,32},{32,0},{64,96},{96,64},{128,160},{160,128},{192,224},{224,1... | collective-permute-start | bytes 1769480 | tf_op jit(solution)/shard_map/ppermute | solution.py:277
  156.1 6.0 %collective-permute-start.1 = (bf16[4,2,6,48,128]{4,3,0,2,1:T(8,128)(2,1)S(1)}, bf16[4,2,6,48,128]{4,3,0,2,1:T(8,128)(2,1)S(1)}, u32[]{:S(2)}, u32[]{:S(2)}) collective-permute-start(bf16[4,2,6,48,128]{4,3,0,2,1:T(8,128)(2,1)S(1)} %copy.18), channel_id=1, source_target_pairs={{0,32},{32,0},{64,96},{96,64},{128,160},{160,128},{192,224},{224,1... | collective-permute-start | bytes 1769480 | tf_op jit(solution)/shard_map/ppermute | solution.py:294
